TPU v7x, 32 devices: a whole 2x2x4 slice. The times are simulated.
32 devices in a mesh: op: 8 (over y, x, core), tm: 4 (over z).
Axes of the slice: x: 2, y: 2, z: 4, core: 2. Of those that a mesh axis runs over, the one named last changes fastest.
Arguments:
- phi: bfloat16 [256, 32, 2, 128, 128], P('op', 'tm'), may hold values from -6 to 6
- tau_fwd: bfloat16 [2, 32, 2, 128, 128], P(None, 'tm'), may hold values from -0.375 to 0.375
- tau_bwd: bfloat16 [2, 32, 2, 128, 128], P(None, 'tm'), may hold values from -0.375 to 0.375
- src_times: int32 [2], replicated, may hold values from 0 to 31
- partner: int32 [256], replicated, may hold values from 0 to 255, each once
Outputs:
- corr: float32 [256, 2, 32, 2, 256], P('op', None, 'tm')
Inputs may be any that keep to these rules, and one draw needn't show every extreme that they name: partner is a permutation of the operators. `src_times`: source times may repeat.
All inputs are finite; a program needn't handle non-finite values.
Results may differ from a plain program's by a relative error of at most 0.0041.
Values may be sent and summed in bfloat16 or wider, within the bound.
No kernel may reach another device: no remote copies, remote signals or barrier semaphores. Data moves between devices by JAX's collectives and lax.ppermute only.
A program may use at most 256 MiB of HBM per device.

v0:
```python
import jax
import jax.numpy as jnp
from jax import lax
from jax.sharding import PartitionSpec as P


def from_root(value, axis, source):
    kept = jnp.where(lax.axis_index(axis) == source, value, 0).astype(value.dtype)
    return lax.psum(kept, axis)


def complex_product(spec, left_re, left_im, right_re, right_im):

    def inner(first, second):
        return jnp.einsum(spec, first, second, preferred_element_type=jnp.float32)

    return (
        inner(left_re, right_re) - inner(left_im, right_im),
        inner(left_re, right_im) + inner(left_im, right_re),
    )


def corr_block(panel, source):
    width = panel.shape[-1]
    sink_re = panel[:, :, :, 0]
    sink_im = panel[:, :, :, 1]
    source_re = source[:, :, 0]
    source_im = source[:, :, 1]

    def inner(first, second):
        return jnp.einsum("jstad,ksad->jstk", first, second, preferred_element_type=jnp.float32)

    real_part = inner(sink_re, source_re) + inner(sink_im, source_im)
    imag_part = inner(sink_im, source_re) - inner(sink_re, source_im)
    return jnp.stack([real_part, imag_part], 3) / width


def body(phi, tau_fwd, tau_bwd, src_times, partner):
    time_local = phi.shape[1]
    sources = tau_fwd.shape[0]
    left_re, left_im = complex_product(
        "stab,jtbc->jstac", tau_fwd[:, :, 0], tau_fwd[:, :, 1], phi[:, :, 0], phi[:, :, 1]
    )
    left_re = left_re.astype(jnp.bfloat16)
    left_im = left_im.astype(jnp.bfloat16)
    sink_re, sink_im = complex_product(
        "jstac,stcd->jstad", left_re, left_im, tau_bwd[:, :, 0], tau_bwd[:, :, 1]
    )
    panel = jnp.stack([sink_re.astype(jnp.bfloat16), sink_im.astype(jnp.bfloat16)], 3)
    fields = []
    for source_index in range(sources):
        when = src_times[source_index]
        local = lax.dynamic_index_in_dim(phi, when % time_local, 1, False)
        fields.append(from_root(local, "tm", when // time_local))
    own_sources = jnp.stack(fields, 1)
    mixed = corr_block(panel, lax.all_gather(own_sources, "op", axis=0, tiled=True))
    return jnp.take(mixed, partner, axis=4)


def solution(mesh):
    in_specs = (
        P("op", "tm", None, None, None),
        P(None, "tm", None, None, None),
        P(None, "tm", None, None, None),
        P(),
        P(),
    )
    out_specs = P("op", None, "tm", None, None)
    return jax.shard_map(body, mesh=mesh, in_specs=in_specs, out_specs=out_specs, check_vma=False)
```

profile of v0, /device:TPU:0, one launch (start us, length us, event | category | flops | bytes accessed | tf_op | source)
XLA Modules:
  0.0 562.1 jit_solution(6328620957796238682)
XLA Ops:
  6.5 0.0 all-reduce.3.cloned.1.call-start
  6.5 1.3 fusion.62
  13.0 2.7 constant_dynamic-slice_fusion.1
  15.8 4.6 copy_select_fusion
  20.4 0.0 all-reduce.3.cloned.1.call-update
  20.4 0.0 all-gather.2.cloned.1.call-start
  20.5 157.8 %all-reduce.3.cloned.1.call-done = (bf16[32,1,2,128,128]{4,0,3,1,2:T(8,128)(2,1)}, bf16[32,1,2,128,128]{4,0,3,1,2:T(8,128)(2,1)}) async-done(((bf16[32,1,2,128,128]{4,0,3,1,2:T(8,128)(2,1)}, bf16[32,1,2,128,128]{4,0,3,1,2:T(8,128)(2,1)}), (bf16[32,1,2,128,128]{4,0,3,1,2:T(8,128)(2,1)}, bf16[32,1,2,128,128]{4,0,3,1,2:T(8,128)(2,1)})) %all-reduce.3.cloned.1.call-update) | async-done | bytes 4194320 | tf_op jit(solution)/shard_map/psum | solution.py:9
  178.3 4.6 pad_maximum_fusion
  182.9 0.0 all-gather.2.cloned.1.call-update
  182.9 13.8 %fusion.60 = (bf16[32,8,1,128,128]{4,3,2,1,0:T(8,128)(2,1)}, bf16[32,8,1,128,128]{4,3,2,1,0:T(8,128)(2,1)}) fusion(bf16[32,8,2,128,128]{4,3,2,1,0:T(8,128)(2,1)} %param.5), kind=kLoop, calls=%fused_computation.59 | loop fusion | bytes 33554432 | tf_op jit(solution)/shard_map/slice | solution.py:42
  196.7 12.1 %copy.63 = bf16[32,8,1,128,128]{3,4,0,1,2:T(8,128)(2,1)} copy(bf16[32,8,1,128,128]{4,3,2,1,0:T(8,128)(2,1)} %get-tuple-element.10) | data formatting | bytes 16777216
  208.9 11.9 %copy.65 = bf16[32,8,1,128,128]{3,4,0,1,2:T(8,128)(2,1)} copy(bf16[32,8,1,128,128]{4,3,2,1,0:T(8,128)(2,1)} %get-tuple-element.9) | data formatting | bytes 16777216
  220.8 0.6 pad_clamp_fusion
  221.4 0.5 compare_and_fusion
  222.0 0.1 fusion.61
  222.1 19.0 %fusion.23 = f32[8,32,128,2,128]{4,2,3,1,0:T(8,128)} fusion(bf16[32,8,1,128,128]{3,4,0,1,2:T(8,128)(2,1)} %copy.63, bf16[2,8,1,128,128]{4,3,2,1,0:T(8,128)(2,1)S(1)} %get-tuple-element.12), kind=kOutput, calls=%fused_computation.26 | convolution fusion | flops 2147483648 | bytes 42467328 | tf_op jit(solution)/shard_map/stab,jtbc->jstac/dot_general | solution.py:15
  241.0 21.0 %fusion.25 = f32[8,32,128,2,128]{4,2,3,1,0:T(8,128)} fusion(bf16[32,8,1,128,128]{3,4,0,1,2:T(8,128)(2,1)} %copy.65, bf16[2,8,1,128,128]{4,3,2,1,0:T(8,128)(2,1)S(1)} %get-tuple-element.12), kind=kOutput, calls=%fused_computation.28 | convolution fusion | flops 2147483648 | bytes 42467328 | tf_op jit(solution)/shard_map/stab,jtbc->jstac/dot_general | solution.py:15
  262.0 20.4 %fusion = bf16[32,2,8,128,128]{3,4,1,0,2:T(8,128)(2,1)} fusion(f32[8,32,128,2,128]{4,2,3,1,0:T(8,128)} %fusion.23, bf16[32,8,1,128,128]{3,4,0,1,2:T(8,128)(2,1)} %copy.65, bf16[2,8,1,128,128]{4,3,2,1,0:T(8,128)(2,1)S(1)} %get-tuple-element.11), kind=kOutput, calls=%fused_computation.5 | convolution fusion | flops 2164260864 | bytes 59244544 | tf_op jit(solution)/shard_map/stab,jtbc->jstac/dot_general | solution.py:15
  282.4 21.5 %fusion.1 = bf16[32,2,8,128,128]{3,4,1,0,2:T(8,128)(2,1)} fusion(f32[8,32,128,2,128]{4,2,3,1,0:T(8,128)} %fusion.25, bf16[32,8,1,128,128]{3,4,0,1,2:T(8,128)(2,1)} %copy.63, bf16[2,8,1,128,128]{4,3,2,1,0:T(8,128)(2,1)S(1)} %get-tuple-element.11), kind=kOutput, calls=%fused_computation.6 | convolution fusion | flops 2164260864 | bytes 59244544 | tf_op jit(solution)/shard_map/stab,jtbc->jstac/dot_general | solution.py:15
  303.9 17.1 %fusion.10 = f32[2,8,32,128,128]{4,3,2,1,0:T(8,128)} fusion(bf16[32,2,8,128,128]{3,4,1,0,2:T(8,128)(2,1)} %fusion, bf16[2,8,2,128,128]{4,3,2,1,0:T(8,128)(2,1)S(1)} %copy-done), kind=kOutput, calls=%fused_computation.17 | convolution fusion | flops 2147483648 | bytes 50855936 | tf_op jit(solution)/shard_map/jstac,stcd->jstad/dot_general | solution.py:15
  320.9 17.1 %fusion.8 = f32[2,8,32,128,128]{4,3,2,1,0:T(8,128)} fusion(bf16[32,2,8,128,128]{3,4,1,0,2:T(8,128)(2,1)} %fusion, bf16[2,8,2,128,128]{4,3,2,1,0:T(8,128)(2,1)S(1)} %copy-done), kind=kOutput, calls=%fused_computation.15 | convolution fusion | flops 2147483648 | bytes 50855936 | tf_op jit(solution)/shard_map/jstac,stcd->jstad/dot_general | solution.py:15
  338.0 25.6 %fusion.16 = bf16[32,2,8,128,128]{4,3,0,2,1:T(8,128)(2,1)} fusion(f32[2,8,32,128,128]{4,3,2,1,0:T(8,128)} %fusion.10, bf16[32,2,8,128,128]{3,4,1,0,2:T(8,128)(2,1)} %fusion.1, bf16[2,8,2,128,128]{4,3,2,1,0:T(8,128)(2,1)S(1)} %copy-done), kind=kOutput, calls=%fused_computation.23 | convolution fusion | flops 2164260864 | bytes 67633152 | tf_op jit(solution)/shard_map/jstac,stcd->jstad/dot_general | solution.py:15
  363.6 23.6 %fusion.19 = bf16[32,2,8,128,128]{4,3,0,2,1:T(8,128)(2,1)} fusion(f32[2,8,32,128,128]{4,3,2,1,0:T(8,128)} %fusion.8, bf16[32,2,8,128,128]{3,4,1,0,2:T(8,128)(2,1)} %fusion.1, bf16[2,8,2,128,128]{4,3,2,1,0:T(8,128)(2,1)S(1)} %copy-done), kind=kOutput, calls=%fused_computation.24 | convolution fusion | flops 2164260864 | bytes 67633152 | tf_op jit(solution)/shard_map/jstac,stcd->jstad/dot_general | solution.py:15
  387.2 39.7 %fusion.31 = f32[2,256,32,8]{1,2,3,0:T(8,128)S(1)} fusion(bf16[32,2,8,128,128]{4,3,0,2,1:T(8,128)(2,1)} %fusion.16, bf16[256,2,2,128,128]{4,0,3,1,2:T(8,128)(2,1)} %all-gather.2.cloned.1.call-done), kind=kOutput, calls=%fused_computation.36 | convolution fusion | flops 4294967296 | bytes 34078720 | tf_op jit(solution)/shard_map/jstad,ksad->jstk/dot_general | solution.py:31
  426.9 39.5 %fusion.28 = f32[2,256,32,8]{1,2,3,0:T(8,128)S(1)} fusion(bf16[32,2,8,128,128]{4,3,0,2,1:T(8,128)(2,1)} %fusion.19, bf16[256,2,2,128,128]{4,0,3,1,2:T(8,128)(2,1)} %all-gather.2.cloned.1.call-done), kind=kOutput, calls=%fused_computation.35 | convolution fusion | flops 4294967296 | bytes 34078720 | tf_op jit(solution)/shard_map/jstad,ksad->jstk/dot_general | solution.py:31
  466.4 39.5 %fusion.43 = f32[32,2,8,1,256]{4,0,2,1,3:T(8,128)S(1)} fusion(f32[2,256,32,8]{1,2,3,0:T(8,128)S(1)} %fusion.31, bf16[32,2,8,128,128]{4,3,0,2,1:T(8,128)(2,1)} %fusion.19, bf16[256,2,2,128,128]{4,0,3,1,2:T(8,128)(2,1)} %all-gather.2.cloned.1.call-done), kind=kOutput, calls=%fused_computation.40 | convolution fusion | flops 4295098368 | bytes 34603008 | tf_op jit(solution)/shard_map/jstad,ksad->jstk/dot_general | solution.py:31
  506.0 32.0 %fusion.49 = f32[32,2,8,1,256]{4,0,2,1,3:T(8,128)S(1)} fusion(f32[2,256,32,8]{1,2,3,0:T(8,128)S(1)} %fusion.28, bf16[32,2,8,128,128]{4,3,0,2,1:T(8,128)(2,1)} %fusion.16, bf16[256,2,2,128,128]{4,0,3,1,2:T(8,128)(2,1)} %all-gather.2.cloned.1.call-done), kind=kOutput, calls=%fused_computation.42 | convolution fusion | flops 4295098368 | bytes 34603008 | tf_op jit(solution)/shard_map/jstad,ksad->jstk/dot_general | solution.py:31
  538.0 0.1 maximum_multiply_fusion
  538.1 2.7 copy.39
  540.8 5.4 gather_fusion
  546.2 4.0 select_bitcast_fusion
  550.2 4.8 copy.40
  (10 shorter events, 0.0 us)
Async XLA Ops:
  6.5 171.8 %all-reduce.3.cloned.1.call-start = ((), (), s32[]{:S(2)}) async-start(), calls=%async_computation.1 | async-start | bytes 8388608 | tf_op jit(solution)/shard_map/psum | solution.py:9
  20.4 366.8 %all-gather.2.cloned.1.call-start = ((), (), s32[]{:S(2)}) async-start(), calls=%async_computation | async-start | bytes 37748736 | tf_op jit(solution)/shard_map/all_gather | solution.py:56
  196.7 24.1 %copy-start.2 = (s32[256]{0:T(256)S(1)}, s32[256]{0:T(256)}, u32[]{:S(2)}) copy-start(s32[256]{0:T(256)} %param.9) | copy-start | bytes 3076
  196.7 25.2 %copy-start.1 = (bf16[2,8,2,128,128]{4,3,2,1,0:T(8,128)(2,1)S(1)}, bf16[2,8,2,128,128]{4,3,2,1,0:T(8,128)(2,1)}, u32[]{:S(2)}) copy-start(bf16[2,8,2,128,128]{4,3,2,1,0:T(8,128)(2,1)} %param.6) | copy-start | bytes 3145732
  282.4 21.5 %copy-start = (bf16[2,8,2,128,128]{4,3,2,1,0:T(8,128)(2,1)S(1)}, bf16[2,8,2,128,128]{4,3,2,1,0:T(8,128)(2,1)}, u32[]{:S(2)}) copy-start(bf16[2,8,2,128,128]{4,3,2,1,0:T(8,128)(2,1)} %param.7) | copy-start | bytes 3145732
  506.0 40.2 %copy-start.3 = (pred[256]{0:T(512)(128)(4,1)S(1)}, pred[256]{0:T(512)(128)(4,1)}, u32[]{:S(2)}) copy-start(pred[256]{0:T(512)(128)(4,1)} %compare_and_fusion) | copy-start | bytes 772
Sparse Core Ops, SparseCore 0:
  20.6 157.7 all-reduce.2
  183.0 166.2 all-gather.1
where the time goes:
time: 567 us; the launch traced here: 562 us
  matrix products  316 us (56%)
  waiting for transfers between devices  158 us (28%)
  local copies, waits for them, and re-layouts  55 us (10%)
  between operations  18.9 us (3%)
  other arithmetic  14.4 us (3%)
    dot_general x8, matrix products, inner(): return jnp.einsum(spec, first, second, preferred_element_type=jnp.float32)  165 us
    psum x1, waiting for transfers between devices, from_root(): return lax.psum(kept, axis)  158 us
    dot_general x4, matrix products, inner(): jnp.einsum('jstad,ksad->jstk', first, second, preferred_element_type=jnp....  151 us
    unnamed x10, local copies, waits for them, and re-layouts  24.1 us
    slice x1, local copies, waits for them, and re-layouts, body(): phi[:, :, 1]  13.8 us
  transfers between devices with their start and end apart: 2, of which 1 were waited for; matrix products, arithmetic and copies ran while one was open for 36% of the time, Pallas kernels for 0%

commit v1 on v0

v1 whole, which is shorter than its diff:
```python
import jax
import jax.numpy as jnp
from jax import lax
from jax.sharding import PartitionSpec as P


def joined(top, low):
    return jnp.concatenate(
        [jnp.concatenate(top, 3), jnp.concatenate(low, 3)], 2
    )


def body(phi, tau_fwd, tau_bwd, src_times, partner):
    ops, time_local = phi.shape[:2]
    sources = tau_fwd.shape[0]
    width = phi.shape[-1]
    here = lax.axis_index("tm")

    fields = []
    for source_index in range(sources):
        when = src_times[source_index]
        local = lax.dynamic_index_in_dim(phi, when % time_local, 1, False)
        fields.append(jnp.where(here == when // time_local, local, 0).astype(phi.dtype))
    own = jnp.stack(fields, 0).transpose(0, 3, 1, 2, 4).reshape(sources * width, ops, 2 * width)
    piece = lax.psum_scatter(own, "tm", scatter_dimension=0, tiled=True)

    left = joined(
        [tau_fwd[:, :, 0], -tau_fwd[:, :, 1]], [tau_fwd[:, :, 1], tau_fwd[:, :, 0]]
    )
    stacked = phi.reshape(ops, time_local, 2 * width, width)
    a = jnp.einsum("stxb,jtbc->stjxc", left, stacked, preferred_element_type=jnp.float32)
    a = a.astype(jnp.bfloat16)
    piece, a = lax.optimization_barrier((piece, a))
    whole = lax.all_gather(piece, ("op", "tm"), axis=0, tiled=True)
    gathered = whole.reshape(-1, sources, width, ops, 2 * width)
    groups = gathered.shape[0]

    a = a.reshape(sources, time_local, ops, 2, width, width)
    a = jnp.concatenate([a[:, :, :, 0], a[:, :, :, 1]], 4)
    back_re, back_im = tau_bwd[:, :, 0], tau_bwd[:, :, 1]
    parts = []
    for right in (
        joined([back_re, back_im], [-back_im, back_re]),
        joined([back_im, -back_re], [back_re, back_im]),
    ):
        p = jnp.einsum("stjac,stcd->stjad", a, right, preferred_element_type=jnp.float32)
        p = p.astype(jnp.bfloat16)
        q = jnp.einsum("stjad,gsakd->jstgk", p, gathered, preferred_element_type=jnp.float32)
        parts.append(q.reshape(ops, sources, time_local, groups * ops))
    q = jnp.stack(parts, 3) / width
    return jnp.take(q, partner, axis=4, mode="clip", unique_indices=True)


def solution(mesh):
    in_specs = (
        P("op", "tm", None, None, None),
        P(None, "tm", None, None, None),
        P(None, "tm", None, None, None),
        P(),
        P(),
    )
    out_specs = P("op", None, "tm", None, None)
    return jax.shard_map(body, mesh=mesh, in_specs=in_specs, out_specs=out_specs, check_vma=False)
```

time: 567 us -> 410 us (0.72)
  matrix products: 316 us -> 149 us
  local copies, waits for them, and re-layouts: 55 us -> 66.7 us
  waiting for transfers between devices: 158 us -> 167 us
  other arithmetic: 14.4 us -> 7.78 us
    dot_general x12 -> x5, matrix products: 316 us -> 149 us  [the longest x2 79.2 us: body(): jnp.einsum('stjad,gsakd->jstgk', p, gathered, preferred_element_type=jnp....]
    psum x1 -> x0, waiting for transfers between devices: 158 us -> none  [from_root(): return lax.psum(kept, axis)]
    all_gather x1, waiting for transfers between devices: 0.01 us -> 112 us  [body(): whole = lax.all_gather(piece, ('op', 'tm'), axis=0, tiled=True)]
    reduce_scatter x0 -> x1, waiting for transfers between devices: none -> 54.9 us  [body(): piece = lax.psum_scatter(own, 'tm', scatter_dimension=0, tiled=True)]
    reshape x0 -> x1, local copies, waits for them, and re-layouts: none -> 7.58 us  [body(): jnp.stack(fields, 0).transpose(0, 3, 1, 2, 4)]
    transpose x0 -> x1, local copies, waits for them, and re-layouts: none -> 6.33 us  [body(): jnp.stack(fields, 0).transpose(0, 3, 1, 2, 4)]
  transfers between devices with their start and end apart: 2 -> 2, of which waited for: 1 -> 2; matrix products, arithmetic and copies ran while one was open for 36% -> 27% of each run, Pallas kernels for 0% -> 0%
where the time goes in v1:
time: 410 us
  waiting for transfers between devices  167 us (41%)
  matrix products  149 us (36%)
  local copies, waits for them, and re-layouts  66.7 us (16%)
  between operations  18.4 us (4%)
  other arithmetic  7.78 us (2%)
    all_gather x1, waiting for transfers between devices, body(): whole = lax.all_gather(piece, ('op', 'tm'), axis=0, tiled=True)  112 us
    dot_general x2, matrix products, body(): jnp.einsum('stjad,gsakd->jstgk', p, gathered, preferred_element_type=jnp....  79.2 us
    reduce_scatter x1, waiting for transfers between devices, body(): piece = lax.psum_scatter(own, 'tm', scatter_dimension=0, tiled=True)  54.9 us
    dot_general x2, matrix products, body(): jnp.einsum('stjac,stcd->stjad', a, right, preferred_element_type=jnp.floa...  46.9 us
    unnamed x10, local copies, waits for them, and re-layouts  24.1 us
    dot_general x1, matrix products, body(): jnp.einsum('stxb,jtbc->stjxc', left, stacked, preferred_element_type=jnp....  23.3 us
    slice x1, local copies, waits for them, and re-layouts, body(): a = jnp.concatenate([a[:, :, :, 0], a[:, :, :, 1]], 4)  13.5 us
    gather x2, local copies, waits for them, and re-layouts, body(): return jnp.take(q, partner, axis=4, mode='clip', unique_indices=True)  10.2 us
  transfers between devices with their start and end apart: 2, of which 2 were waited for; matrix products, arithmetic and copies ran while one was open for 27% of the time, Pallas kernels for 0%

profile of v1, /device:TPU:0, one launch (start us, length us, event | category | flops | bytes accessed | tf_op | source)
XLA Modules:
  0.0 409.7 jit_solution(11897296104286786696)
XLA Ops:
  6.5 1.3 fusion.65
  12.7 1.7 fusion.44
  14.5 1.7 fusion.43
  16.2 0.4 maximum_bitcast_fusion
  16.6 6.3 %copy.48 = bf16[2,128,32,2,128]{4,3,2,1,0:T(2,128)(2,1)} copy(bf16[2,128,32,2,128]{4,1,3,2,0:T(8,128)(2,1)S(1)} %maximum_bitcast_fusion) | data formatting | bytes 8388608 | tf_op jit(solution)/shard_map/transpose | solution.py:24
  23.0 7.6 %reshape.38 = bf16[256,32,256]{2,1,0:T(8,128)(2,1)} reshape(bf16[2,128,32,2,128]{4,3,2,1,0:T(2,128)(2,1)} %copy.48) | data formatting | bytes 8388608 | tf_op jit(solution)/shard_map/reshape | solution.py:24
  30.5 0.0 reduce-scatter.2.cloned.1.call-update
  30.6 0.2 all-gather.2.cloned.1.call-start
  30.8 1.0 copy-done.1
  31.8 0.1 fusion.64
  31.9 0.1 fusion.62
  31.9 0.1 copy_bitcast_fusion.2
  32.1 0.0 copy-start.3
  32.1 23.3 %convert_bitcast_fusion = bf16[2,8,32,256,128]{4,3,2,0,1:T(8,128)(2,1)} fusion(bf16[32,8,256,128,1]{3,2,1,0,4:T(8,128)(2,1)} %bitcast.110, bf16[2,8,128,128]{3,2,0,1:T(8,128)(2,1)S(1)} %get-tuple-element.20, bf16[2,8,128,128]{3,2,0,1:T(8,128)(2,1)S(1)} %get-tuple-element.19, bf16[2,8,128,128]{3,2,0,1:T(8,128)(2,1)S(1)} %fusion.62), kind=kOutput, calls=%fused_computation.8 | convolution fusion | flops 8615100416 | bytes 51904512 | tf_op jit(solution)/shard_map/stxb,jtbc->stjxc/dot_general | solution.py:31
  55.4 54.9 %reduce-scatter.2.cloned.1.call-done = bf16[64,32,256]{2,1,0:T(8,128)(2,1)} async-done(((bf16[256,32,256]{2,1,0:T(8,128)(2,1)}), bf16[64,32,256]{2,1,0:T(8,128)(2,1)}) %reduce-scatter.2.cloned.1.call-update) | async-done | bytes 1048592 | tf_op jit(solution)/shard_map/reduce_scatter | solution.py:25
  110.2 0.0 all-gather.2.cloned.1.call-update
  110.3 0.6 pad_clamp_fusion
  110.9 0.1 slice_bitcast_fusion.1
  110.9 0.9 fusion.61
  111.9 13.5 %fusion.63 = (bf16[2,8,32,1,128,128]{5,4,3,2,0,1:T(8,128)(2,1)S(1)}, bf16[2,8,32,1,128,128]{5,4,3,2,0,1:T(8,128)(2,1)S(1)}) fusion(bf16[2,8,32,2,128,128]{5,4,3,2,0,1:T(8,128)(2,1)} %bitcast.109), kind=kLoop, calls=%fused_computation.56 | loop fusion | bytes 67108864 | tf_op jit(solution)/shard_map/slice | solution.py:39
  125.4 11.6 %copy.107 = bf16[2,8,32,1,128,128]{5,2,4,1,0,3:T(8,128)(2,1)} copy(bf16[2,8,32,1,128,128]{5,4,3,2,0,1:T(8,128)(2,1)S(1)} %get-tuple-element.10) | data formatting | bytes 33554432
  137.0 11.6 %copy.108 = bf16[2,8,32,1,128,128]{5,2,4,1,0,3:T(8,128)(2,1)} copy(bf16[2,8,32,1,128,128]{5,4,3,2,0,1:T(8,128)(2,1)S(1)} %get-tuple-element.9) | data formatting | bytes 33554432
  148.6 23.4 %fusion.69 = bf16[2,8,32,128,256,1]{4,2,3,1,5,0:T(8,128)(2,1)} fusion(bf16[2,8,32,128,128]{4,2,3,1,0:T(8,128)(2,1)} %bitcast.111, bf16[2,8,32,128,128]{4,2,3,1,0:T(8,128)(2,1)} %bitcast.113, bf16[2,8,128,128]{3,2,1,0:T(8,128)(2,1)S(1)} %get-tuple-element.13, bf16[2,8,128,128]{3,2,1,0:T(8,128)(2,1)S(1)} %copy-done.2, ...), kind=kOutput, calls=%fused_computation.5.clone.clone.clone.1 | convolution fusion | flops 8682209280 | bytes 68681728 | tf_op jit(solution)/shard_map/stjac,stcd->stjad/dot_general | solution.py:46
  172.0 23.5 %fusion.71 = bf16[2,8,32,128,256,1]{4,2,3,1,5,0:T(8,128)(2,1)} fusion(bf16[2,8,32,128,128]{4,2,3,1,0:T(8,128)(2,1)} %bitcast.112, bf16[2,8,32,128,128]{4,2,3,1,0:T(8,128)(2,1)} %bitcast.114, bf16[2,8,128,128]{3,2,1,0:T(8,128)(2,1)S(1)} %get-tuple-element.14, bf16[2,8,128,128]{3,2,1,0:T(8,128)(2,1)S(1)} %get-tuple-element.13, ...), kind=kOutput, calls=%fused_computation.3.clone.clone.clone | convolution fusion | flops 8682209280 | bytes 68681728 | tf_op jit(solution)/shard_map/stjac,stcd->stjad/dot_general | solution.py:46
  195.5 112.4 %all-gather.2.cloned.1.call-done = bf16[2048,32,256]{2,1,0:T(8,128)(2,1)} async-done(((bf16[64,32,256]{2,1,0:T(8,128)(2,1)}), bf16[2048,32,256]{2,1,0:T(8,128)(2,1)}) %all-gather.2.cloned.1.call-update) | async-done | bytes 33554448 | tf_op jit(solution)/shard_map/all_gather | solution.py:34
  307.9 39.6 %fusion.45 = f32[32,2,8,8,32]{0,4,2,3,1:T(8,128)S(1)} fusion(bf16[8,2,128,32,256,1]{4,3,2,1,0,5:T(8,128)(2,1)} %bitcast.118, bf16[2,8,32,128,256,1]{4,2,3,1,5,0:T(8,128)(2,1)} %fusion.69), kind=kOutput, calls=%fused_computation.43 | convolution fusion | flops 8589934592 | bytes 67633152 | tf_op jit(solution)/shard_map/stjad,gsakd->jstgk/dot_general | solution.py:48
  347.5 1.6 copy.77
  349.1 39.6 %fusion.50 = f32[32,2,8,8,32]{0,4,2,3,1:T(8,128)S(1)} fusion(bf16[8,2,128,32,256,1]{4,3,2,1,0,5:T(8,128)(2,1)} %bitcast.119, bf16[2,8,32,128,256,1]{4,2,3,1,5,0:T(8,128)(2,1)} %fusion.71), kind=kOutput, calls=%fused_computation.44 | convolution fusion | flops 8589934592 | bytes 67633152 | tf_op jit(solution)/shard_map/stjad,gsakd->jstgk/dot_general | solution.py:48
  388.7 1.6 copy.80
  390.4 2.3 maximum_multiply_fusion
  392.7 5.4 %gather_fusion = f32[256,32,2,8,2]{1,3,4,2,0:T(8,128)} fusion(f32[32,2,8,2,256]{0,2,4,3,1:T(8,128)} %maximum_multiply_fusion, s32[1024]{0:T(1024)} %pad_clamp_fusion), kind=kCustom, calls=%fused_computation | custom fusion | bytes 2098176 | tf_op jit(solution)/shard_map/jit(_take)/gather | solution.py:51
  398.1 4.8 %copy.62 = f32[32,2,8,2,256]{4,3,2,1,0:T(2,128)} copy(f32[32,2,8,2,256]{0,2,3,1,4:T(8,128)} %bitcast.117) | data formatting | bytes 2097152 | tf_op jit(solution)/shard_map/jit(_take)/gather | solution.py:51
  (7 shorter events, 0.0 us)
Async XLA Ops:
  6.5 103.7 %reduce-scatter.2.cloned.1.call-start = ((), (), s32[]{:S(2)}) async-start(), calls=%async_computation.1 | async-start | bytes 5242880 | tf_op jit(solution)/shard_map/reduce_scatter | solution.py:25
  30.5 1.2 copy-start.1
  30.6 277.3 %all-gather.2.cloned.1.call-start = ((), (), s32[]{:S(2)}) async-start(), calls=%async_computation.2 | async-start | bytes 34603008 | tf_op jit(solution)/shard_map/all_gather | solution.py:34
  32.1 78.2 %copy-start.3 = (s32[256]{0:T(256)S(1)}, s32[256]{0:T(256)}, u32[]{:S(2)}) copy-start(s32[256]{0:T(256)} %param.9) | copy-start | bytes 3076
  32.1 78.8 %copy-start = (bf16[2,8,2,128,128]{4,3,2,1,0:T(8,128)(2,1)S(1)}, bf16[2,8,2,128,128]{4,3,2,1,0:T(8,128)(2,1)}, u32[]{:S(2)}) copy-start(bf16[2,8,2,128,128]{4,3,2,1,0:T(8,128)(2,1)} %param.7) | copy-start | bytes 3145732
  137.0 11.6 %copy-start.2 = (bf16[2,8,128,128]{3,2,1,0:T(8,128)(2,1)S(1)}, bf16[2,8,128,128]{3,2,1,0:T(8,128)(2,1)}, u32[]{:S(2)}) copy-start(bf16[2,8,128,128]{3,2,1,0:T(8,128)(2,1)} %get-tuple-element.11) | copy-start | bytes 1572868
Sparse Core Ops, SparseCore 0:
  30.7 79.5 reduce-scatter.1
  113.2 194.6 all-gather.1
